TPU v7x, 32 devices: a whole 2x2x4 slice. The times are simulated.
32 devices in a mesh: expert: 8 (over z, y), vocab: 4 (over x, core).
Axes of the slice: x: 2, y: 2, z: 4, core: 2. Of those that a mesh axis runs over, the one named last changes fastest.
Arguments:
- layer_out: bfloat16 [256, 2048], P('expert'), may hold values from -6 to 6
- moe_input: bfloat16 [256, 2048], P('expert'), may hold values from -6 to 6
- final_gain: float32 [2048], replicated, may hold values from 0.1 to 1.9
- head_weight: bfloat16 [2048, 12288], P(None, ('expert', 'vocab')), may hold values from -0.125 to 0.125
- clean_ids: int32 [256], P('expert'), may hold values from 0 to 12287
- levels: int32 [256], P('expert'), may hold values from 0 to 15
- ratio_table: float32 [16], replicated, may hold values from 0.5 to 8
- gate_weights: float32 [256, 8], P('expert'), may hold values from 0.05 to 0.5
- expert_ids: int32 [256, 8], P('expert'), may hold values from 0 to 15, all different within a row; in each aligned block of 32 rows (0 to 31, 32 to 63, ...) at most 32 rows name the same one
- w_gate: bfloat16 [16, 2048, 1024], P('expert', None, 'vocab'), may hold values from -0.125 to 0.125
- w_up: bfloat16 [16, 2048, 1024], P('expert', None, 'vocab'), may hold values from -0.125 to 0.125
- w_down: bfloat16 [16, 1024, 2048], P('expert', 'vocab'), may hold values from -0.1875 to 0.1875
Outputs:
- head_grad: float32 [2048, 12288], P(None, ('expert', 'vocab'))
- residual_grad: float32 [256, 2048], P('expert', 'vocab')
- input_grad: float32 [256, 2048], P('expert', 'vocab')
Inputs may be any that keep to these rules, and one draw needn't show every extreme that they name: `expert_ids`: the 8 experts of a row are distinct; among the 32 rows of one index of expert no expert is named by more than 32 rows.
All inputs are finite; a program needn't handle non-finite values.
Results may differ from a plain program's by a relative error of at most 0.0044.
The roundings to bfloat16 on the way count: a program that leaves them out, or rounds other values in their place, can miss the bound.
Values may be sent and summed in bfloat16 or wider, within the bound.
A program may use at most 64 MiB of HBM per device.

v0:
```python
import math
import jax
import jax.numpy as jnp
from jax import lax
from jax.sharding import PartitionSpec as P

epsilon = 1e-05


def on_device(
    layer_out,
    moe_input,
    final_gain,
    head_weight,
    clean_ids,
    levels,
    ratio_table,
    gate_weights,
    expert_ids,
    w_gate,
    w_up,
    w_down,
):
    rows_local, model_width = layer_out.shape
    top_count = expert_ids.shape[1]
    n_expert = lax.axis_size("expert")
    n_vocab = lax.axis_size("vocab")
    total_rows = rows_local * n_expert
    local_experts = w_gate.shape[0]
    experts_all = local_experts * n_expert
    capacity = max(2, 2 * rows_local * top_count // experts_all)
    feature_share = model_width // n_vocab
    vocab_local = head_weight.shape[1]
    values = layer_out.astype(jnp.float32)
    row_scale = jnp.sqrt(jnp.mean(values * values, axis=1, keepdims=True) + epsilon)
    unit_rows = values / row_scale
    normed = (unit_rows * final_gain[None, :]).astype(jnp.bfloat16)
    normed_all, clean_all, level_all = (
        lax.all_gather(normed, "expert", axis=0, tiled=True),
        lax.all_gather(clean_ids, "expert", axis=0, tiled=True),
        lax.all_gather(levels, "expert", axis=0, tiled=True),
    )
    level_labels = jnp.arange(ratio_table.shape[0], dtype=jnp.int32)
    ratio_rows = jnp.sum(
        jnp.where(level_all[:, None] == level_labels[None, :], ratio_table[None, :], 0.0), axis=1
    )
    column_start = (lax.axis_index("expert") * n_vocab + lax.axis_index("vocab")) * vocab_local
    columns = column_start + jnp.arange(vocab_local, dtype=jnp.int32)
    scores = jnp.dot(normed_all, head_weight, preferred_element_type=jnp.float32)
    target_hit = (clean_all[:, None] == columns[None, :]).astype(jnp.float32)
    loss_scale = 1.0 / math.sqrt(total_rows)
    score_grad = ((jnp.exp(scores) - ratio_rows[:, None] * target_hit) * loss_scale).astype(
        jnp.bfloat16
    )
    head_grad = lax.dot_general(
        normed_all, score_grad, (((0,), (0,)), ((), ())), preferred_element_type=jnp.float32
    )
    partial_grad = lax.psum_scatter(
        lax.dot_general(
            score_grad, head_weight, (((1,), (1,)), ((), ())), preferred_element_type=jnp.float32
        ),
        "expert",
        scatter_dimension=0,
        tiled=True,
    )
    normed_grad = lax.psum(partial_grad, "vocab")
    gained = final_gain[None, :] * normed_grad
    residual_full = (
        gained - unit_rows * jnp.mean(unit_rows * gained, axis=1, keepdims=True)
    ) / row_scale
    feature_start = lax.axis_index("vocab") * feature_share
    residual_grad = lax.dynamic_slice_in_dim(residual_full, feature_start, feature_share, 1)
    flat_ids = expert_ids.reshape(-1)
    labels = jnp.arange(experts_all, dtype=jnp.int32)
    onehot = (flat_ids[:, None] == labels[None, :]).astype(jnp.int32)
    earlier = jnp.cumsum(onehot, axis=0) - onehot
    slot_index = jnp.sum(earlier * onehot, axis=1)
    position = flat_ids * capacity + slot_index
    routed_grad = (
        (gate_weights[:, :, None] * residual_full[:, None, :])
        .astype(jnp.bfloat16)
        .reshape(-1, model_width)
    )
    inputs_rep = jnp.repeat(moe_input, top_count, axis=0)
    buffer_rows = experts_all * capacity
    send_inputs = (
        jnp.zeros((buffer_rows, model_width), jnp.bfloat16)
        .at[position]
        .set(inputs_rep)
        .reshape(experts_all, capacity, model_width)
    )
    send_grads = (
        jnp.zeros((buffer_rows, model_width), jnp.bfloat16)
        .at[position]
        .set(routed_grad)
        .reshape(experts_all, capacity, model_width)
    )
    part_inputs = lax.dynamic_slice_in_dim(send_inputs, feature_start, feature_share, 2)
    part_grads = lax.dynamic_slice_in_dim(send_grads, feature_start, feature_share, 2)
    moved_inputs, moved_grads = (
        lax.all_to_all(part_inputs, "expert", split_axis=0, concat_axis=1, tiled=True),
        lax.all_to_all(part_grads, "expert", split_axis=0, concat_axis=1, tiled=True),
    )
    inputs_slot, grads_slot = (
        lax.all_gather(moved_inputs, "vocab", axis=2, tiled=True),
        lax.all_gather(moved_grads, "vocab", axis=2, tiled=True),
    )
    gate_pre = jnp.einsum("esd,edf->esf", inputs_slot, w_gate, preferred_element_type=jnp.float32)
    up_pre = jnp.einsum("esd,edf->esf", inputs_slot, w_up, preferred_element_type=jnp.float32)
    act_grad = jnp.einsum("esd,efd->esf", grads_slot, w_down, preferred_element_type=jnp.float32)
    sigmoid_gate = jax.nn.sigmoid(gate_pre)
    gate_grad = (act_grad * up_pre * sigmoid_gate * (1.0 + gate_pre * (1.0 - sigmoid_gate))).astype(
        jnp.bfloat16
    )
    up_grad = (act_grad * gate_pre * sigmoid_gate).astype(jnp.bfloat16)
    partial_input = jnp.einsum(
        "esf,edf->esd", gate_grad, w_gate, preferred_element_type=jnp.float32
    )
    partial_input = partial_input + jnp.einsum(
        "esf,edf->esd", up_grad, w_up, preferred_element_type=jnp.float32
    )
    slot_share = lax.psum_scatter(partial_input, "vocab", scatter_dimension=2, tiled=True)
    returned = lax.all_to_all(slot_share, "expert", split_axis=1, concat_axis=0, tiled=True)
    per_pair = returned.reshape(-1, feature_share)[position]
    input_grad = jnp.sum(per_pair.reshape(rows_local, top_count, feature_share), axis=1)
    return (head_grad, residual_grad, input_grad)


def solution(mesh):
    in_specs = (
        P("expert", None),
        P("expert", None),
        P(),
        P(None, ("expert", "vocab")),
        P("expert"),
        P("expert"),
        P(),
        P("expert", None),
        P("expert", None),
        P("expert", None, "vocab"),
        P("expert", None, "vocab"),
        P("expert", "vocab", None),
    )
    out_specs = (P(None, ("expert", "vocab")), P("expert", "vocab"), P("expert", "vocab"))
    return jax.shard_map(
        on_device, mesh=mesh, in_specs=in_specs, out_specs=out_specs, check_vma=False
    )
```

profile of v0, /device:TPU:0, one launch (start us, length us, event | category | flops | bytes accessed | tf_op | source)
XLA Modules:
  0.0 321.3 jit_solution(14341958270852453572)
XLA Ops:
  7.2 1.2 fusion.20
  8.4 1.7 multiply_convert_fusion.2
  10.2 1.2 dynamic-slice
  12.1 0.9 dynamic-update-slice
  13.8 13.1 %all-reduce.2 = (s32[256]{0:T(256)S(1)}, s32[256]{0:T(256)S(1)}) all-reduce(s32[256]{0:T(256)S(1)} %dynamic-update-slice.1, s32[256]{0:T(256)S(1)} %dynamic-update-slice), channel_id=1, replica_groups=mesh['expert'=8,'vocab'=4] {'expert'}, use_global_device_ids=true, to_apply=%add.1 | all-reduce | flops 512 | bytes 4096
  27.7 26.3 %all-gather.4.cloned.1.call-done = bf16[256,2048]{1,0:T(8,128)(2,1)} async-done(((bf16[32,2048]{1,0:T(8,128)(2,1)}), bf16[256,2048]{1,0:T(8,128)(2,1)}) %all-gather.4.cloned.1.call-update) | async-done | bytes 1048592 | tf_op jit(solution)/shard_map/all_gather | solution.py:39
  53.9 2.6 fusion.6
  57.2 2.1 fusion.30
  60.7 3.7 %scatter_custom_fusion.1 = bf16[512,2048]{1,0:T(8,128)(2,1)} fusion(s32[256]{0:T(256)S(1)} %bitcast.68, bf16[]{:T(256)} %constant.39.clone.1, bf16[32,2048]{1,0:T(8,128)(2,1)S(1)} %copy-done.5), kind=kCustom, calls=%fused_computation.16 | custom fusion | bytes 2228226 | tf_op jit(solution)/shard_map/scatter | solution.py:89
  64.4 2.0 constant_dynamic-slice_fusion
  66.4 3.5 %all-to-all-start.1 = ((bf16[16,32,512]{2,1,0:T(8,128)(2,1)}), bf16[16,32,512]{2,1,0:T(8,128)(2,1)S(1)}, u32[]{:S(2)}, u32[]{:S(2)}) async-start(bf16[16,32,512]{2,1,0:T(8,128)(2,1)} %constant_dynamic-slice_fusion), calls=%async_computation.2 | async-start | bytes 1048576 | tf_op jit(solution)/shard_map/all_to_all | solution.py:101
  70.0 64.0 %reduce-scatter.3.cloned.1.call-done = f32[32,2048]{1,0:T(8,128)} async-done(((f32[256,2048]{1,0:T(8,128)}), f32[32,2048]{1,0:T(8,128)}) %reduce-scatter.3.cloned.1.call-update) | async-done | bytes 262160 | tf_op jit(solution)/shard_map/reduce_scatter | solution.py:58
  135.1 32.5 %all-reduce.5.cloned.1.call-done = f32[32,2048]{1,0:T(8,128)} async-done(((f32[32,2048]{1,0:T(8,128)}), f32[32,2048]{1,0:T(8,128)}) %all-reduce.5.cloned.1.call-update) | async-done | bytes 262160 | tf_op jit(solution)/shard_map/psum | solution.py:66
  167.6 1.2 multiply_reduce_fusion
  168.8 1.1 subtract_divide_fusion
  169.9 3.8 %scatter_custom_fusion = bf16[512,2048]{1,0:T(8,128)(2,1)} fusion(s32[256]{0:T(256)S(1)} %bitcast.69, f32[32,2048]{1,0:T(8,128)S(1)} %subtract_divide_fusion, f32[256]{0:T(256)S(1)} %mul.124, bf16[]{:T(256)} %constant.39.clone.1), kind=kCustom, calls=%fused_computation.15 | custom fusion | flops 1048576 | bytes 2360322 | tf_op jit(solution)/shard_map/scatter | solution.py:95
  173.7 1.1 constant_dynamic-slice_fusion.1
  174.7 18.6 %all_to_all.51 = bf16[16,32,512]{2,1,0:T(8,128)(2,1)S(1)} all-to-all(bf16[16,32,512]{2,1,0:T(8,128)(2,1)S(1)} %constant_dynamic-slice_fusion.1), channel_id=1, replica_groups=mesh['expert'=8,'vocab'=4] {'expert'}, dimensions={0} | all-to-all | bytes 1048576 | tf_op jit(solution)/shard_map/all_to_all | solution.py:102
  194.5 2.9 fusion.32
  197.4 18.8 %all-gather.6.cloned.1.call-done = bf16[2,256,2048]{2,1,0:T(8,128)(2,1)} async-done(((bf16[2,256,512]{2,1,0:T(8,128)(2,1)}), bf16[2,256,2048]{2,1,0:T(8,128)(2,1)}) %all-gather.6.cloned.1.call-update) | async-done | bytes 2097168 | tf_op jit(solution)/shard_map/all_gather | solution.py:106
  216.2 3.0 fusion.31
  219.2 5.6 %fusion.7 = f32[2,256,2048]{2,1,0:T(8,128)} fusion(bf16[2,2048,256]{2,1,0:T(8,128)(2,1)} %param.21, f32[2,256,256]{2,1,0:T(8,128)S(1)} %fusion.31, bf16[2,256,2048]{2,1,0:T(8,128)(2,1)} %all-gather.8.cloned.1.call-done, bf16[2,2048,256]{2,1,0:T(8,128)(2,1)S(1)} %copy-done, f32[2,256,256]{2,1,0:T(8,128)S(1)} %fusion.32), kind=kOutput, calls=%fused_computation.14 | convolution fusion | flops 1075052544 | bytes 11534336 | tf_op jit(solution)/shard_map/esf,edf->esd/dot_general | solution.py:116
  224.8 4.9 %convolution_add_fusion = f32[2,256,2048]{2,1,0:T(8,128)} fusion(f32[2,256,2048]{2,1,0:T(8,128)} %fusion.7, bf16[2,2048,256]{2,1,0:T(8,128)(2,1)S(1)} %copy-done, f32[2,256,256]{2,1,0:T(8,128)S(1)} %fusion.31, f32[2,256,256]{2,1,0:T(8,128)S(1)} %fusion.32), kind=kOutput, calls=%fused_computation.3 | convolution fusion | flops 538705920 | bytes 11534336 | tf_op jit(solution)/shard_map/esf,edf->esd/dot_general | solution.py:119
  229.7 44.6 %reduce-scatter.5.cloned.1.call-done = f32[2,256,512]{2,1,0:T(8,128)} async-done(((f32[2,256,2048]{2,1,0:T(8,128)}), f32[2,256,512]{2,1,0:T(8,128)}) %reduce-scatter.5.cloned.1.call-update) | async-done | bytes 1048592 | tf_op jit(solution)/shard_map/reduce_scatter | solution.py:122
  274.2 3.0 copy.40
  277.3 5.5 %all-to-all-start.2 = ((f32[2,256,512]{2,0,1:T(2,128)}), f32[2,256,512]{2,0,1:T(2,128)S(1)}, u32[]{:S(2)}, u32[]{:S(2)}) async-start(f32[2,256,512]{2,0,1:T(2,128)} %copy.40), calls=%async_computation.4 | async-start | bytes 2097152 | tf_op jit(solution)/shard_map/all_to_all | solution.py:123
  282.8 3.7 %fusion.29 = f32[2048,384]{1,0:T(8,128)} fusion(bf16[256,2048]{1,0:T(8,128)(2,1)} %all-gather.4.cloned.1.call-done, bf16[256,384]{1,0:T(8,128)(2,1)} %copy-done.4), kind=kOutput, calls=%fused_computation.59 | convolution fusion | flops 402653184 | bytes 4390912 | tf_op jit(solution)/shard_map/dot_general | solution.py:55
  287.1 21.4 %all-to-all-done.2 = f32[2,256,512]{2,0,1:T(2,128)S(1)} async-done(((f32[2,256,512]{2,0,1:T(2,128)}), f32[2,256,512]{2,0,1:T(2,128)S(1)}, u32[]{:S(2)}, u32[]{:S(2)}) %all-to-all-start.2) | async-done | bytes 1048608 | tf_op jit(solution)/shard_map/all_to_all | solution.py:123
  308.5 1.0 copy-done.1
  309.4 1.4 copy.41
  310.9 1.8 gather_fusion
  312.6 1.8 bitcast_reduce_fusion
  (57 shorter events, 6.7 us)
Async XLA Ops:
  7.2 212.0 %copy-start = (bf16[2,2048,256]{2,1,0:T(8,128)(2,1)S(1)}, bf16[2,2048,256]{2,1,0:T(8,128)(2,1)}, u32[]{:S(2)}) copy-start(bf16[2,2048,256]{2,1,0:T(8,128)(2,1)} %param.22) | copy-start | bytes 6291460
  7.2 46.7 %all-gather.4.cloned.1.call-start = ((), (), s32[]{:S(2)}) async-start(), calls=%async_computation.5 | async-start | bytes 1179648 | tf_op jit(solution)/shard_map/all_gather | solution.py:39
  10.1 123.8 %reduce-scatter.3.cloned.1.call-start = ((), (), s32[]{:S(2)}) async-start(), calls=%async_computation.6 | async-start | bytes 2359296 | tf_op jit(solution)/shard_map/reduce_scatter | solution.py:58
  53.9 3.3 %copy-start.3 = (bf16[2048,384]{1,0:T(8,128)(2,1)S(1)}, bf16[2048,384]{1,0:T(8,128)(2,1)}, u32[]{:S(2)}) copy-start(bf16[2048,384]{1,0:T(8,128)(2,1)} %param.15) | copy-start | bytes 4718596
  56.5 0.7 copy-start.4
  57.2 2.1 copy-start.7
  59.2 1.4 copy-start.5
  64.4 70.6 %copy-start.8 = (f32[32,8]{0,1:T(8,128)S(1)}, f32[32,8]{0,1:T(8,128)}, u32[]{:S(2)}) copy-start(f32[32,8]{0,1:T(8,128)} %param.19) | copy-start | bytes 3076
  64.4 103.2 %copy-start.2 = (bf16[32,2048]{1,0:T(8,128)(2,1)S(1)}, bf16[32,2048]{1,0:T(8,128)(2,1)}, u32[]{:S(2)}) copy-start(bf16[32,2048]{1,0:T(8,128)(2,1)} %param.12) | copy-start | bytes 393220
  64.4 103.2 %copy-start.6 = (f32[2048]{0:T(1024)S(1)}, f32[2048]{0:T(1024)}, u32[]{:S(2)}) copy-start(f32[2048]{0:T(1024)} %param.14) | copy-start | bytes 24580
  66.4 67.6 %all-to-all-start.1 = ((bf16[16,32,512]{2,1,0:T(8,128)(2,1)}), bf16[16,32,512]{2,1,0:T(8,128)(2,1)S(1)}, u32[]{:S(2)}, u32[]{:S(2)}) async-start(bf16[16,32,512]{2,1,0:T(8,128)(2,1)} %constant_dynamic-slice_fusion), calls=%async_computation.2 | async-start | bytes 1048576 | tf_op jit(solution)/shard_map/all_to_all | solution.py:101
  69.9 97.7 %all-reduce.5.cloned.1.call-start = ((), (), s32[]{:S(2)}) async-start(), calls=%async_computation.7 | async-start | bytes 524288 | tf_op jit(solution)/shard_map/psum | solution.py:66
  134.0 60.5 %all-gather.8.cloned.1.call-start = ((), (), s32[]{:S(2)}) async-start(), calls=%async_computation.9 | async-start | bytes 2621440 | tf_op jit(solution)/shard_map/all_gather | solution.py:105
  134.9 81.3 %all-gather.6.cloned.1.call-start = ((), (), s32[]{:S(2)}) async-start(), calls=%async_computation.8 | async-start | bytes 2621440 | tf_op jit(solution)/shard_map/all_gather | solution.py:106
  194.2 80.0 %reduce-scatter.5.cloned.1.call-start = ((), (), s32[]{:S(2)}) async-start(), calls=%async_computation.10 | async-start | bytes 5242880 | tf_op jit(solution)/shard_map/reduce_scatter | solution.py:122
  277.3 31.2 %all-to-all-start.2 = ((f32[2,256,512]{2,0,1:T(2,128)}), f32[2,256,512]{2,0,1:T(2,128)S(1)}, u32[]{:S(2)}, u32[]{:S(2)}) async-start(f32[2,256,512]{2,0,1:T(2,128)} %copy.40), calls=%async_computation.4 | async-start | bytes 2097152 | tf_op jit(solution)/shard_map/all_to_all | solution.py:123
  308.4 1.0 copy-start.1
Sparse Core Ops, SparseCore 0:
  10.7 43.1 all-gather.3
  59.4 74.5 reduce-scatter.2
  136.3 31.2 all-reduce.4
  169.0 22.5 all-gather.7
  194.4 21.8 all-gather.5
  229.8 44.4 reduce-scatter.4
where the time goes:
time: 322 us; the launch traced here: 321 us
  waiting for transfers between devices  208 us (65%)
  blocking collectives  31.8 us (10%)
  matrix products  24.6 us (8%)
  local copies, waits for them, and re-layouts  20.8 us (6%)
  between operations  14.9 us (5%)
  other arithmetic  12.2 us (4%)
  starting transfers between devices  9.43 us (3%)
    reduce_scatter x1, waiting for transfers between devices, on_device(): lax.psum_scatter(lax.dot_general(score_grad, head_weight, (((1,), (1,)),...  64 us
    reduce_scatter x1, waiting for transfers between devices, on_device(): lax.psum_scatter(partial_input, 'vocab', scatter_dimension=2, tiled=True)  44.6 us
    psum x1, waiting for transfers between devices, on_device(): normed_grad = lax.psum(partial_grad, 'vocab')  32.5 us
    all_gather x1, waiting for transfers between devices, on_device(): lax.all_gather(normed, 'expert', axis=0, tiled=True)  26.3 us
    all_to_all x1, waiting for transfers between devices, on_device(): lax.all_to_all(slot_share, 'expert', split_axis=1, concat_axis=0, tiled=T...  21.4 us
    all_gather x1, waiting for transfers between devices, on_device(): lax.all_gather(moved_grads, 'vocab', axis=2, tiled=True)  18.8 us
    all_to_all x1, blocking collectives, on_device(): lax.all_to_all(part_grads, 'expert', split_axis=0, concat_axis=1, tiled=T...  18.6 us
    unnamed x1, blocking collectives  13.1 us
  transfers between devices with their start and end apart: 8, of which 6 were waited for; matrix products, arithmetic and copies ran while one was open for 8% of the time, Pallas kernels for 0%

commit v1 on v0

--- a/solution.py
+++ b/solution.py
@@ -63,7 +63,7 @@
         scatter_dimension=0,
         tiled=True,
     )
-    normed_grad = lax.psum(partial_grad, "vocab")
+    normed_grad = jnp.sum(lax.all_gather(partial_grad, "vocab"), axis=0)
     gained = final_gain[None, :] * normed_grad
     residual_full = (
         gained - unit_rows * jnp.mean(unit_rows * gained, axis=1, keepdims=True)

time: 322 us -> 302 us (0.938)
  waiting for transfers between devices: 208 us -> 177 us
  blocking collectives: 31.8 us -> 46.9 us
  starting transfers between devices: 9.43 us -> 5.94 us
    psum x1 -> x0, waiting for transfers between devices: 32.5 us -> none  [on_device(): normed_grad = lax.psum(partial_grad, 'vocab')]
    all_to_all x0 -> x1, blocking collectives: none -> 16.5 us  [on_device(): lax.all_to_all(part_inputs, 'expert', split_axis=0, concat_axis=1, tiled=...]
    all_to_all x1 -> x0, starting transfers between devices: 3.49 us -> none  [on_device(): lax.all_to_all(part_inputs, 'expert', split_axis=0, concat_axis=1, tiled=...]
  transfers between devices with their start and end apart: 8 -> 7, of which waited for: 6 -> 5; matrix products, arithmetic and copies ran while one was open for 8% -> 8% of each run, Pallas kernels for 0% -> 0%
where the time goes in v1:
time: 302 us; the launch traced here: 301 us
  waiting for transfers between devices  177 us (59%)
  blocking collectives  46.9 us (16%)
  matrix products  24.6 us (8%)
  local copies, waits for them, and re-layouts  19.8 us (7%)
  between operations  15 us (5%)
  other arithmetic  11.6 us (4%)
  starting transfers between devices  5.94 us (2%)
    reduce_scatter x1, waiting for transfers between devices, on_device(): lax.psum_scatter(lax.dot_general(score_grad, head_weight, (((1,), (1,)),...  66.1 us
    reduce_scatter x1, waiting for transfers between devices, on_device(): lax.psum_scatter(partial_input, 'vocab', scatter_dimension=2, tiled=True)  44.6 us
    all_gather x1, waiting for transfers between devices, on_device(): lax.all_gather(normed, 'expert', axis=0, tiled=True)  26.3 us
    all_to_all x1, waiting for transfers between devices, on_device(): lax.all_to_all(slot_share, 'expert', split_axis=1, concat_axis=0, tiled=T...  21.4 us
    all_gather x1, waiting for transfers between devices, on_device(): lax.all_gather(moved_grads, 'vocab', axis=2, tiled=True)  18.6 us
    all_to_all x1, blocking collectives, on_device(): lax.all_to_all(part_grads, 'expert', split_axis=0, concat_axis=1, tiled=T...  17.3 us
    all_to_all x1, blocking collectives, on_device(): lax.all_to_all(part_inputs, 'expert', split_axis=0, concat_axis=1, tiled=...  16.5 us
    unnamed x1, blocking collectives  13.1 us
  transfers between devices with their start and end apart: 7, of which 5 were waited for; matrix products, arithmetic and copies ran while one was open for 8% of the time, Pallas kernels for 0%

profile of v1, /device:TPU:0, one launch (start us, length us, event | category | flops | bytes accessed | tf_op | source)
XLA Modules:
  0.0 300.9 jit_solution(13419283740276331426)
XLA Ops:
  7.2 1.2 fusion.20
  8.4 1.7 multiply_convert_fusion.2
  10.2 1.2 dynamic-slice
  12.1 0.9 dynamic-update-slice
  13.0 0.8 dynamic-update-slice.1
  13.8 13.1 %all-reduce.2 = (s32[256]{0:T(256)S(1)}, s32[256]{0:T(256)S(1)}) all-reduce(s32[256]{0:T(256)S(1)} %dynamic-update-slice.1, s32[256]{0:T(256)S(1)} %dynamic-update-slice), channel_id=1, replica_groups=mesh['expert'=8,'vocab'=4] {'expert'}, use_global_device_ids=true, to_apply=%add.1 | all-reduce | flops 512 | bytes 4096
  27.7 26.3 %all-gather.6.cloned.1.call-done = bf16[256,2048]{1,0:T(8,128)(2,1)} async-done(((bf16[32,2048]{1,0:T(8,128)(2,1)}), bf16[256,2048]{1,0:T(8,128)(2,1)}) %all-gather.6.cloned.1.call-update) | async-done | bytes 1048592 | tf_op jit(solution)/shard_map/all_gather | solution.py:39
  53.9 2.6 fusion.6
  57.2 2.1 fusion.30
  60.4 66.1 %reduce-scatter.3.cloned.1.call-done = f32[32,2048]{1,0:T(8,128)} async-done(((f32[256,2048]{1,0:T(8,128)}), f32[32,2048]{1,0:T(8,128)}) %reduce-scatter.3.cloned.1.call-update) | async-done | bytes 262160 | tf_op jit(solution)/shard_map/reduce_scatter | solution.py:58
  126.9 3.7 %scatter_custom_fusion.1 = bf16[512,2048]{1,0:T(8,128)(2,1)} fusion(s32[256]{0:T(256)S(1)} %bitcast.70, bf16[]{:T(256)} %constant.39.clone.1, bf16[32,2048]{1,0:T(8,128)(2,1)S(1)} %copy-done.5), kind=kCustom, calls=%fused_computation.16 | custom fusion | bytes 2228226 | tf_op jit(solution)/shard_map/scatter | solution.py:89
  130.6 1.1 constant_dynamic-slice_fusion
  131.7 16.5 %all_to_all.51 = bf16[16,32,512]{2,1,0:T(8,128)(2,1)S(1)} all-to-all(bf16[16,32,512]{2,1,0:T(8,128)(2,1)S(1)} %constant_dynamic-slice_fusion), channel_id=1, replica_groups=mesh['expert'=8,'vocab'=4] {'expert'}, dimensions={0} | all-to-all | bytes 1048576 | tf_op jit(solution)/shard_map/all_to_all | solution.py:101
  148.2 0.8 copy.39
  149.3 1.3 reduce_sum.58
  151.0 3.8 %scatter_custom_fusion = bf16[512,2048]{1,0:T(8,128)(2,1)} fusion(s32[256]{0:T(256)S(1)} %bitcast.71, f32[32,2048]{1,0:T(8,128)S(1)} %subtract_divide_fusion, f32[256]{0:T(256)S(1)} %mul.124, bf16[]{:T(256)} %constant.39.clone.1), kind=kCustom, calls=%fused_computation.15 | custom fusion | flops 1048576 | bytes 2360322 | tf_op jit(solution)/shard_map/scatter | solution.py:95
  154.8 1.1 constant_dynamic-slice_fusion.1
  155.9 17.3 %all_to_all.52 = bf16[16,32,512]{2,1,0:T(8,128)(2,1)S(1)} all-to-all(bf16[16,32,512]{2,1,0:T(8,128)(2,1)S(1)} %constant_dynamic-slice_fusion.1), channel_id=1, replica_groups=mesh['expert'=8,'vocab'=4] {'expert'}, dimensions={0} | all-to-all | bytes 1048576 | tf_op jit(solution)/shard_map/all_to_all | solution.py:102
  174.3 2.9 fusion.32
  177.3 18.6 %all-gather.8.cloned.1.call-done = bf16[2,256,2048]{2,1,0:T(8,128)(2,1)} async-done(((bf16[2,256,512]{2,1,0:T(8,128)(2,1)}), bf16[2,256,2048]{2,1,0:T(8,128)(2,1)}) %all-gather.8.cloned.1.call-update) | async-done | bytes 2097168 | tf_op jit(solution)/shard_map/all_gather | solution.py:106
  195.8 3.0 fusion.31
  198.8 5.6 %fusion.7 = f32[2,256,2048]{2,1,0:T(8,128)} fusion(bf16[2,2048,256]{2,1,0:T(8,128)(2,1)} %param.21, f32[2,256,256]{2,1,0:T(8,128)S(1)} %fusion.31, bf16[2,256,2048]{2,1,0:T(8,128)(2,1)} %all-gather.10.cloned.1.call-done, bf16[2,2048,256]{2,1,0:T(8,128)(2,1)S(1)} %copy-done, f32[2,256,256]{2,1,0:T(8,128)S(1)} %fusion.32), kind=kOutput, calls=%fused_computation.14 | convolution fusion | flops 1075052544 | bytes 11534336 | tf_op jit(solution)/shard_map/esf,edf->esd/dot_general | solution.py:116
  204.4 4.9 %convolution_add_fusion = f32[2,256,2048]{2,1,0:T(8,128)} fusion(f32[2,256,2048]{2,1,0:T(8,128)} %fusion.7, bf16[2,2048,256]{2,1,0:T(8,128)(2,1)S(1)} %copy-done, f32[2,256,256]{2,1,0:T(8,128)S(1)} %fusion.31, f32[2,256,256]{2,1,0:T(8,128)S(1)} %fusion.32), kind=kOutput, calls=%fused_computation.3 | convolution fusion | flops 538705920 | bytes 11534336 | tf_op jit(solution)/shard_map/esf,edf->esd/dot_general | solution.py:119
  209.3 44.6 %reduce-scatter.5.cloned.1.call-done = f32[2,256,512]{2,1,0:T(8,128)} async-done(((f32[2,256,2048]{2,1,0:T(8,128)}), f32[2,256,512]{2,1,0:T(8,128)}) %reduce-scatter.5.cloned.1.call-update) | async-done | bytes 1048592 | tf_op jit(solution)/shard_map/reduce_scatter | solution.py:122
  253.9 3.0 %copy.40 = f32[2,256,512]{2,0,1:T(2,128)} copy(f32[2,256,512]{2,1,0:T(8,128)} %reduce-scatter.5.cloned.1.call-done) | data formatting | bytes 2097152 | tf_op jit(solution)/shard_map/reduce_scatter | solution.py:122
  256.9 5.5 %all-to-all-start.2 = ((f32[2,256,512]{2,0,1:T(2,128)}), f32[2,256,512]{2,0,1:T(2,128)S(1)}, u32[]{:S(2)}, u32[]{:S(2)}) async-start(f32[2,256,512]{2,0,1:T(2,128)} %copy.40), calls=%async_computation.4 | async-start | bytes 2097152 | tf_op jit(solution)/shard_map/all_to_all | solution.py:123
  262.4 3.7 %fusion.29 = f32[2048,384]{1,0:T(8,128)} fusion(bf16[256,2048]{1,0:T(8,128)(2,1)} %all-gather.6.cloned.1.call-done, bf16[256,384]{1,0:T(8,128)(2,1)} %copy-done.4), kind=kOutput, calls=%fused_computation.59 | convolution fusion | flops 402653184 | bytes 4390912 | tf_op jit(solution)/shard_map/dot_general | solution.py:55
  266.7 21.4 %all-to-all-done.2 = f32[2,256,512]{2,0,1:T(2,128)S(1)} async-done(((f32[2,256,512]{2,0,1:T(2,128)}), f32[2,256,512]{2,0,1:T(2,128)S(1)}, u32[]{:S(2)}, u32[]{:S(2)}) %all-to-all-start.2) | async-done | bytes 1048608 | tf_op jit(solution)/shard_map/all_to_all | solution.py:123
  288.1 1.0 copy-done.1
  289.1 1.4 copy.41
  290.5 1.8 gather_fusion
  292.2 1.8 bitcast_reduce_fusion
  (57 shorter events, 5.4 us)
Async XLA Ops:
  7.2 191.6 %copy-start = (bf16[2,2048,256]{2,1,0:T(8,128)(2,1)S(1)}, bf16[2,2048,256]{2,1,0:T(8,128)(2,1)}, u32[]{:S(2)}) copy-start(bf16[2,2048,256]{2,1,0:T(8,128)(2,1)} %param.22) | copy-start | bytes 6291460
  7.2 46.7 %all-gather.6.cloned.1.call-start = ((), (), s32[]{:S(2)}) async-start(), calls=%async_computation.5 | async-start | bytes 1179648 | tf_op jit(solution)/shard_map/all_gather | solution.py:39
  10.1 116.4 %reduce-scatter.3.cloned.1.call-start = ((), (), s32[]{:S(2)}) async-start(), calls=%async_computation.6 | async-start | bytes 2359296 | tf_op jit(solution)/shard_map/reduce_scatter | solution.py:58
  53.9 3.3 %copy-start.3 = (bf16[2048,384]{1,0:T(8,128)(2,1)S(1)}, bf16[2048,384]{1,0:T(8,128)(2,1)}, u32[]{:S(2)}) copy-start(bf16[2048,384]{1,0:T(8,128)(2,1)} %param.15) | copy-start | bytes 4718596
  56.5 0.7 copy-start.4
  57.2 2.1 copy-start.7
  59.2 67.6 %copy-start.5 = (bf16[32,2048]{1,0:T(8,128)(2,1)S(1)}, bf16[32,2048]{1,0:T(8,128)(2,1)}, u32[]{:S(2)}) copy-start(bf16[32,2048]{1,0:T(8,128)(2,1)} %param.13) | copy-start | bytes 393220
  59.3 90.0 %all-gather.12.cloned.1.call-start = ((), (), s32[]{:S(2)}) async-start(), calls=%async_computation.10 | async-start | bytes 1310720 | tf_op jit(solution)/shard_map/all_gather | solution.py:66
  126.6 47.7 %all-gather.10.cloned.1.call-start = ((), (), s32[]{:S(2)}) async-start(), calls=%async_computation.8 | async-start | bytes 2621440 | tf_op jit(solution)/shard_map/all_gather | solution.py:105
  130.6 18.5 %copy-start.8 = (f32[32,8]{0,1:T(8,128)S(1)}, f32[32,8]{0,1:T(8,128)}, u32[]{:S(2)}) copy-start(f32[32,8]{0,1:T(8,128)} %param.19) | copy-start | bytes 3076
  131.7 18.9 %copy-start.2 = (bf16[32,2048]{1,0:T(8,128)(2,1)S(1)}, bf16[32,2048]{1,0:T(8,128)(2,1)}, u32[]{:S(2)}) copy-start(bf16[32,2048]{1,0:T(8,128)(2,1)} %param.12) | copy-start | bytes 393220
  131.7 18.9 %copy-start.6 = (f32[2048]{0:T(1024)S(1)}, f32[2048]{0:T(1024)}, u32[]{:S(2)}) copy-start(f32[2048]{0:T(1024)} %param.14) | copy-start | bytes 24580
  149.1 46.8 %all-gather.8.cloned.1.call-start = ((), (), s32[]{:S(2)}) async-start(), calls=%async_computation.7 | async-start | bytes 2621440 | tf_op jit(solution)/shard_map/all_gather | solution.py:106
  174.1 79.8 %reduce-scatter.5.cloned.1.call-start = ((), (), s32[]{:S(2)}) async-start(), calls=%async_computation.9 | async-start | bytes 5242880 | tf_op jit(solution)/shard_map/reduce_scatter | solution.py:122
  256.9 31.2 %all-to-all-start.2 = ((f32[2,256,512]{2,0,1:T(2,128)}), f32[2,256,512]{2,0,1:T(2,128)S(1)}, u32[]{:S(2)}, u32[]{:S(2)}) async-start(f32[2,256,512]{2,0,1:T(2,128)} %copy.40), calls=%async_computation.4 | async-start | bytes 2097152 | tf_op jit(solution)/shard_map/all_to_all | solution.py:123
  288.1 1.0 copy-start.1
Sparse Core Ops, SparseCore 0:
  10.7 43.1 all-gather.5
  59.4 67.1 reduce-scatter.2
  128.1 15.6 all-gather.11
  149.2 21.6 all-gather.9
  174.2 21.6 all-gather.7
  209.4 44.4 reduce-scatter.4
